TPU v7x, 256 devices: a 8x8x2 block of a 8x8x16 slice. The times are simulated.
256 devices in a mesh: group: 2 (over z), dp: 16 (over y, core), tensor: 8 (over x).
Axes of the slice: x: 8, y: 8, z: 2, core: 2. Of those that a mesh axis runs over, the one named last changes fastest.
The devices are a block of a 8x8x16 slice.
Arguments:
- tokens: bfloat16 [4096, 5120], P(('group', 'dp'), 'tensor'), parts along dimension 0, may hold values from -6 to 6
- router: bfloat16 [5120, 8], replicated, may hold values from -0.078125 to 0.078125
- expert_gate: bfloat16 [5120, 32768], P(None, ('dp', 'tensor')), may hold values from -0.078125 to 0.078125
- expert_up: bfloat16 [5120, 32768], P(None, ('dp', 'tensor')), may hold values from -0.078125 to 0.078125
- expert_down: bfloat16 [32768, 5120], P(('dp', 'tensor')), may hold values from -0.09375 to 0.09375
- shared_gate: bfloat16 [5120, 4096], P('dp', 'tensor'), may hold values from -0.078125 to 0.078125
- shared_up: bfloat16 [5120, 4096], P('dp', 'tensor'), may hold values from -0.078125 to 0.078125
- shared_down: bfloat16 [4096, 5120], P('tensor', 'dp'), may hold values from -0.09375 to 0.09375
- expert_ids: int32 [4096], P(('group', 'dp')), parts along dimension 0, may hold values from 0 to 7, as said below
- expert_slots: int32 [4096], P(('group', 'dp')), parts along dimension 0, may hold values from 0 to 31, as said below
Outputs:
- mixed: bfloat16 [4096, 5120], P(('group', 'dp'), 'tensor'), parts along dimension 0
There are 2 independent parts, one for each index of `group`. A program takes and returns all parts, laid end to end along the dimension named above; an argument that names none is the same for every part. Nothing has to cross between parts.
Inputs may be any that keep to these rules, and one draw needn't show every extreme that they name: `expert_ids`: among the tokens of one index of dp no expert has more than 32; in every draw one expert has exactly 32 tokens from every index of dp. `expert_slots`: tokens of one index of dp with the same expert have distinct slots.
All inputs are finite; a program needn't handle non-finite values.
Results may differ from a plain program's by a relative error of at most 0.015.
Values may be sent and summed in bfloat16 or wider, within the bound.
No kernel may reach another device: no remote copies, remote signals or barrier semaphores. Data moves between devices by JAX's collectives and lax.ppermute only.
A program may use at most 128 MiB of HBM per device.

v0:
```python
import jax
import jax.numpy as jnp
from jax import lax
from jax.sharding import PartitionSpec as P


def joined_along(tiles, dim):
    dims = list(tiles.shape[1:])
    dims[dim] *= tiles.shape[0]
    return jnp.moveaxis(tiles, 0, dim).reshape(dims)


def copy_for_each(value, axis):
    copies = jnp.broadcast_to(value, (lax.axis_size(axis), *value.shape))
    return lax.all_to_all(copies, axis, split_axis=0, concat_axis=0, tiled=True)


def gather_directly(value, axis, dim):
    return joined_along(copy_for_each(value, axis), dim)


def side_by_side(arrays, axis, dim, along):
    both = jnp.concatenate(arrays, axis=along)
    out, at, finished = (lax.all_gather(both, axis, axis=dim, tiled=True), 0, [])
    for a in arrays:
        finished.append(lax.slice_in_dim(out, at, at + a.shape[along], axis=along))
        at += a.shape[along]
    return tuple(finished)


def split_up(value, dim, devices):
    before, after = (value.shape[:dim], value.shape[dim + 1 :])
    return jnp.moveaxis(value.reshape(*before, devices, -1, *after), dim, 0)


def sum_at_owner(value, axis, dim):
    tiles = split_up(value, dim, lax.axis_size(axis))
    arrived = lax.all_to_all(tiles, axis, split_axis=0, concat_axis=0, tiled=True)
    return arrived.astype(jnp.float32).sum(axis=0)


def swapped(value, axis, bit):
    mask = 2**bit
    pairs = [(source, source ^ mask) for source in range(lax.axis_size(axis))]
    return lax.ppermute(value, axis, pairs)


def on_device(
    tokens,
    router,
    expert_gate,
    expert_up,
    expert_down,
    shared_gate,
    shared_up,
    shared_down,
    expert_ids,
    expert_slots,
):
    tok_rows, part_width = tokens.shape
    dp_count = lax.axis_size("dp")
    experts = dp_count // 2
    capacity = min(2 * tok_rows // experts, tok_rows // 2)
    gathered = gather_directly(tokens, "tensor", 1)
    logits = jnp.dot(gathered, router, preferred_element_type=jnp.float32)
    one_hot = (expert_ids[:, None] == jnp.arange(experts, dtype=jnp.int32)[None, :]).astype(
        jnp.float32
    )
    gating = jax.nn.sigmoid(jnp.sum(logits * one_hot, axis=1))
    routed = (tokens.astype(jnp.float32) * gating[:, None]).astype(jnp.bfloat16)
    outgoing = (
        jnp.zeros((experts, capacity, part_width), jnp.bfloat16)
        .at[expert_ids, expert_slots]
        .set(routed)
    )
    pieces = side_by_side((shared_gate, shared_up), "dp", 0, 1)
    gate_sum = jnp.dot(gathered, pieces[0], preferred_element_type=jnp.float32)
    up_sum = jnp.dot(gathered, pieces[1], preferred_element_type=jnp.float32)
    shared_hidden = (jax.nn.silu(gate_sum) * up_sum).astype(jnp.bfloat16)
    shared_terms = jnp.dot(
        shared_hidden,
        lax.all_gather(shared_down, "dp", axis=1, tiled=True),
        preferred_element_type=jnp.float32,
    )
    shared_out = lax.psum_scatter(
        shared_terms.astype(jnp.bfloat16), "tensor", scatter_dimension=1, tiled=True
    ).astype(jnp.float32)
    half_cap = capacity // 2
    to_send = outgoing.reshape(dp_count, half_cap, part_width)
    own_half = lax.all_to_all(to_send, "dp", split_axis=0, concat_axis=0, tiled=True)
    partner = swapped(own_half, "dp", 0)
    parity = lax.axis_index("dp") % 2
    odd_host = parity == 1
    lower_half = jnp.where(odd_host, partner, own_half)
    upper_half = jnp.where(odd_host, own_half, partner)
    received = jnp.concatenate([lower_half, upper_half], axis=1)
    source_count = received.shape[0]
    slot_count = received.shape[1]
    slot_total = source_count * slot_count
    portion = lax.all_gather(received, "tensor", axis=2, tiled=True)
    flattened = portion.reshape(slot_total, portion.shape[2])
    gate_e = jnp.dot(flattened, expert_gate, preferred_element_type=jnp.float32)
    up_e = jnp.dot(flattened, expert_up, preferred_element_type=jnp.float32)
    hidden_e = (jax.nn.silu(gate_e) * up_e).astype(jnp.bfloat16)
    expert_terms = jnp.dot(hidden_e, expert_down, preferred_element_type=jnp.float32)
    expert_terms = expert_terms.reshape(source_count, slot_count, expert_terms.shape[1])
    partials = sum_at_owner(expert_terms.astype(jnp.bfloat16), "tensor", 2)
    partner_sum = swapped(partials.astype(jnp.bfloat16), "dp", 0).astype(partials.dtype)
    paired = partials + partner_sum
    kept_half = lax.dynamic_slice_in_dim(paired, parity * half_cap, half_cap, 1).astype(
        jnp.bfloat16
    )
    returned_raw = lax.all_to_all(kept_half, "dp", split_axis=0, concat_axis=0, tiled=True)
    returned = returned_raw.reshape(experts, capacity, part_width)
    expert_out = returned[expert_ids, expert_slots]
    return (shared_out + expert_out.astype(jnp.float32)).astype(jnp.bfloat16)


def solution(mesh):
    in_specs = (
        P(("group", "dp"), "tensor"),
        P(),
        P(None, ("dp", "tensor")),
        P(None, ("dp", "tensor")),
        P(("dp", "tensor"), None),
        P("dp", "tensor"),
        P("dp", "tensor"),
        P("tensor", "dp"),
        P(("group", "dp")),
        P(("group", "dp")),
    )
    out_specs = P(("group", "dp"), "tensor")
    return jax.shard_map(
        on_device, mesh=mesh, in_specs=in_specs, out_specs=out_specs, check_vma=False
    )
```

profile of v0, /device:TPU:515, one launch (start us, length us, event | category | flops | bytes accessed | tf_op | source)
XLA Modules:
  0.0 342.5 jit_solution(5509344661017308061)
XLA Ops:
  6.6 1.2 copy.12
  7.8 1.3 broadcast_in_dim.8
  9.0 7.2 %all-to-all-start = ((bf16[8,128,640]{1,2,0:T(8,128)(2,1)}), bf16[8,128,640]{1,2,0:T(8,128)(2,1)}, u32[]{:S(2)}, u32[]{:S(2)}) async-start(bf16[8,128,640]{1,2,0:T(8,128)(2,1)} %broadcast_in_dim.8), calls=%async_computation | async-start | bytes 2621440 | tf_op jit(solution)/shard_map/all_to_all | solution.py:15
  16.2 19.5 %all-to-all-done = bf16[8,128,640]{1,2,0:T(8,128)(2,1)} async-done(((bf16[8,128,640]{1,2,0:T(8,128)(2,1)}), bf16[8,128,640]{1,2,0:T(8,128)(2,1)}, u32[]{:S(2)}, u32[]{:S(2)}) %all-to-all-start) | async-done | bytes 1310752 | tf_op jit(solution)/shard_map/all_to_all | solution.py:15
  35.7 1.6 fusion.17
  37.5 8.0 %scatter_fusion = bf16[8,32,640]{2,1,0:T(8,128)(2,1)S(1)} fusion(bf16[8,32,640]{2,1,0:T(8,128)(2,1)S(1)} %broadcast_in_dim.18, s32[128]{0:T(128)S(1)} %get-tuple-element.8, bf16[128,640]{1,0:T(8,128)(2,1)S(1)} %multiply_convert_fusion), kind=kCustom, calls=%fused_computation.1 | custom fusion | bytes 492544 | tf_op jit(solution)/shard_map/scatter | solution.py:74
  45.5 40.7 %all_to_all.20 = bf16[16,16,640]{2,1,0:T(8,128)(2,1)S(1)} all-to-all(bf16[16,16,640]{2,1,0:T(8,128)(2,1)S(1)} %bitcast.60), channel_id=1, replica_groups=mesh['group'=2,'dp'=16,'tensor'=8] {'dp'}, dimensions={0} | all-to-all | bytes 655360 | tf_op jit(solution)/shard_map/all_to_all | solution.py:90
  86.2 1.6 collective-permute-done
  87.9 0.9 pad_maximum_fusion.1
  88.9 2.0 pad_maximum_fusion
  91.0 0.7 all-gather.6.cloned.1.call-update
  91.7 63.9 %all-gather.8.cloned.1.call-done = bf16[16,32,5120]{2,1,0:T(8,128)(2,1)} async-done(((bf16[16,32,640]{2,1,0:T(8,128)(2,1)}), bf16[16,32,5120]{2,1,0:T(8,128)(2,1)}) %all-gather.8.cloned.1.call-update) | async-done | bytes 5242896 | tf_op jit(solution)/shard_map/all_gather | solution.py:100
  155.6 4.8 %fusion.40 = f32[512,256]{1,0:T(8,128)S(1)} fusion(bf16[512,5120]{1,0:T(8,128)(2,1)} %bitcast.65, bf16[5120,256]{1,0:T(8,128)(2,1)} %param.12), kind=kOutput, calls=%fused_computation.52 | convolution fusion | flops 1342177280 | bytes 8388608 | tf_op jit(solution)/shard_map/dot_general | solution.py:102
  160.5 11.2 %convolution_convert_fusion = bf16[512,5120]{1,0:T(8,128)(2,1)} fusion(bf16[256,5120]{1,0:T(8,128)(2,1)S(1)} %copy-done, bf16[512,5120]{1,0:T(8,128)(2,1)} %bitcast.66, bf16[5120,256]{1,0:T(8,128)(2,1)} %param.13, f32[512,256]{1,0:T(8,128)S(1)} %fusion.40), kind=kOutput, calls=%fused_computation.3 | convolution fusion | flops 2687762432 | bytes 16252928 | tf_op jit(solution)/shard_map/dot_general | solution.py:105
  171.7 3.7 %copy.16 = bf16[64,8,8,640]{3,2,1,0:T(8,128)(2,1)S(1)} copy(bf16[64,8,8,640]{3,1,2,0:T(8,128)(2,1)} %bitcast.62) | data formatting | bytes 10485760
  175.3 3.1 copy.18
  178.4 6.2 %all-to-all-start.2 = ((bf16[8,16,32,640]{3,2,1,0:T(8,128)(2,1)}), bf16[8,16,32,640]{3,2,1,0:T(8,128)(2,1)}, u32[]{:S(2)}, u32[]{:S(2)}) async-start(bf16[8,16,32,640]{3,2,1,0:T(8,128)(2,1)} %bitcast.58), calls=%async_computation.2 | async-start | bytes 10485760 | tf_op jit(solution)/shard_map/all_to_all | solution.py:38
  184.6 41.0 %all-gather.4.cloned.1.call-done = bf16[5120,1024]{1,0:T(8,128)(2,1)} async-done(((bf16[320,1024]{1,0:T(8,128)(2,1)}), bf16[5120,1024]{1,0:T(8,128)(2,1)}) %all-gather.4.cloned.1.call-update) | async-done | bytes 10485776 | tf_op jit(solution)/shard_map/all_gather | solution.py:24
  225.6 4.4 %fusion.5 = f32[128,512]{0,1:T(8,128)S(1)} fusion(bf16[128,5120]{0,1:T(8,128)(2,1)} %bitcast.1, bf16[5120,1024]{1,0:T(8,128)(2,1)} %all-gather.4.cloned.1.call-done), kind=kOutput, calls=%fused_computation.12 | convolution fusion | flops 671088640 | bytes 6815744 | tf_op jit(solution)/shard_map/dot_general | solution.py:77
  230.1 40.7 %all-gather.6.cloned.1.call-done = bf16[512,5120]{0,1:T(8,128)(2,1)} async-done(((bf16[512,320]{0,1:T(8,128)(2,1)}), bf16[512,5120]{0,1:T(8,128)(2,1)}) %all-gather.6.cloned.1.call-update) | async-done | bytes 5242896 | tf_op jit(solution)/shard_map/all_gather | solution.py:82
  270.7 11.2 %convolution_convert_fusion.1 = bf16[128,5120]{1,0:T(8,128)(2,1)} fusion(bf16[512,5120]{0,1:T(8,128)(2,1)} %all-gather.6.cloned.1.call-done, bf16[128,5120]{0,1:T(8,128)(2,1)} %bitcast.1, bf16[5120,1024]{1,0:T(8,128)(2,1)} %all-gather.4.cloned.1.call-done, f32[128,512]{0,1:T(8,128)S(1)} %fusion.5), kind=kOutput, calls=%fused_computation.4 | convolution fusion | flops 1343225856 | bytes 13369344 | tf_op jit(solution)/shard_map/dot_general | solution.py:80
  281.9 2.4 copy.14
  284.4 17.9 %all-to-all-done.2 = bf16[8,16,32,640]{3,2,1,0:T(8,128)(2,1)} async-done(((bf16[8,16,32,640]{3,2,1,0:T(8,128)(2,1)}), bf16[8,16,32,640]{3,2,1,0:T(8,128)(2,1)}, u32[]{:S(2)}, u32[]{:S(2)}) %all-to-all-start.2) | async-done | bytes 5242912 | tf_op jit(solution)/shard_map/all_to_all | solution.py:38
  302.4 3.4 %convert_reduce_fusion = f32[16,32,640]{2,1,0:T(8,128)S(1)} fusion(bf16[8,16,32,640]{3,2,1,0:T(8,128)(2,1)} %all-to-all-done.2), kind=kLoop, calls=%fused_computation.2 | loop fusion | flops 4915200 | bytes 6553600 | tf_op jit(solution)/shard_map/reduce_sum | solution.py:39
  305.8 1.1 copy-done.1
  307.0 2.7 collective-permute-start.1
  309.7 1.9 collective-permute-done.1
  311.5 2.0 fusion.20
  313.5 7.4 %all-to-all-start.3 = ((bf16[16,16,640]{2,1,0:T(8,128)(2,1)}), bf16[16,16,640]{2,1,0:T(8,128)(2,1)S(1)}, u32[]{:S(2)}, u32[]{:S(2)}) async-start(bf16[16,16,640]{2,1,0:T(8,128)(2,1)} %fusion.20), calls=%async_computation.3 | async-start | bytes 655360 | tf_op jit(solution)/shard_map/all_to_all | solution.py:113
  320.9 1.1 copy.15
  322.0 11.9 %all-to-all-done.3 = bf16[16,16,640]{2,1,0:T(8,128)(2,1)S(1)} async-done(((bf16[16,16,640]{2,1,0:T(8,128)(2,1)}), bf16[16,16,640]{2,1,0:T(8,128)(2,1)S(1)}, u32[]{:S(2)}, u32[]{:S(2)}) %all-to-all-start.3) | async-done | bytes 327712 | tf_op jit(solution)/shard_map/all_to_all | solution.py:113
  333.9 1.4 gather_fusion
  (27 shorter events, 1.3 us)
Async XLA Ops:
  6.5 153.9 %copy-start = (bf16[256,5120]{1,0:T(8,128)(2,1)S(1)}, bf16[256,5120]{1,0:T(8,128)(2,1)}, u32[]{:S(2)}) copy-start(bf16[256,5120]{1,0:T(8,128)(2,1)} %param.14) | copy-start | bytes 7864324
  6.6 9.7 %copy-start.4 = (s32[128]{0:T(128)S(1)}, s32[128]{0:T(128)}, u32[]{:S(2)}) copy-start(s32[128]{0:T(128)} %param.18) | copy-start | bytes 1540
  6.6 9.7 %copy-start.5 = (s32[128]{0:T(128)S(1)}, s32[128]{0:T(128)}, u32[]{:S(2)}) copy-start(s32[128]{0:T(128)} %param.19) | copy-start | bytes 1540
  6.6 29.1 %copy-start.3 = (bf16[5120,8]{0,1:T(8,128)(2,1)S(1)}, bf16[5120,8]{0,1:T(8,128)(2,1)}, u32[]{:S(2)}) copy-start(bf16[5120,8]{0,1:T(8,128)(2,1)} %param.11) | copy-start | bytes 245764
  7.8 29.5 %copy-start.2 = (bf16[128,640]{1,0:T(8,128)(2,1)S(1)}, bf16[128,640]{1,0:T(8,128)(2,1)}, u32[]{:S(2)}) copy-start(bf16[128,640]{1,0:T(8,128)(2,1)} %param.10) | copy-start | bytes 491524
  9.0 26.6 %all-to-all-start = ((bf16[8,128,640]{1,2,0:T(8,128)(2,1)}), bf16[8,128,640]{1,2,0:T(8,128)(2,1)}, u32[]{:S(2)}, u32[]{:S(2)}) async-start(bf16[8,128,640]{1,2,0:T(8,128)(2,1)} %broadcast_in_dim.8), calls=%async_computation | async-start | bytes 2621440 | tf_op jit(solution)/shard_map/all_to_all | solution.py:15
  16.2 139.4 %all-gather.8.cloned.1.call-start = ((), (), s32[]{:S(2)}) async-start(), calls=%async_computation.7 | async-start | bytes 5898240 | tf_op jit(solution)/shard_map/all_gather | solution.py:100
  86.2 1.6 collective-permute-start
  88.8 136.8 %all-gather.4.cloned.1.call-start = ((), (), s32[]{:S(2)}) async-start(), calls=%async_computation.5 | async-start | bytes 11141120 | tf_op jit(solution)/shard_map/all_gather | solution.py:24
  90.9 179.8 %all-gather.6.cloned.1.call-start = ((), (), s32[]{:S(2)}) async-start(), calls=%async_computation.6 | async-start | bytes 5570560 | tf_op jit(solution)/shard_map/all_gather | solution.py:82
  178.4 124.0 %all-to-all-start.2 = ((bf16[8,16,32,640]{3,2,1,0:T(8,128)(2,1)}), bf16[8,16,32,640]{3,2,1,0:T(8,128)(2,1)}, u32[]{:S(2)}, u32[]{:S(2)}) async-start(bf16[8,16,32,640]{3,2,1,0:T(8,128)(2,1)} %bitcast.58), calls=%async_computation.2 | async-start | bytes 10485760 | tf_op jit(solution)/shard_map/all_to_all | solution.py:38
  184.6 136.3 %reduce-scatter.4.cloned.1.call-start = ((), (), s32[]{:S(2)}) async-start(), calls=%async_computation.8 | async-start | bytes 1474560
  305.8 1.1 copy-start.1
  307.0 4.6 %collective-permute-start.1 = (bf16[16,32,640]{2,1,0:T(8,128)(2,1)S(1)}, bf16[16,32,640]{2,1,0:T(8,128)(2,1)}, u32[]{:S(2)}, u32[]{:S(2)}) collective-permute-start(bf16[16,32,640]{2,1,0:T(8,128)(2,1)S(1)} %convert_element_type.53), channel_id=1, source_target_pairs={{0,8},{8,0},{16,24},{24,16},{32,40},{40,32},{48,56},{56,48},{64,72... | collective-permute-start | bytes 1966088 | tf_op jit(solution)/shard_map/ppermute | solution.py:45
  313.5 20.4 %all-to-all-start.3 = ((bf16[16,16,640]{2,1,0:T(8,128)(2,1)}), bf16[16,16,640]{2,1,0:T(8,128)(2,1)S(1)}, u32[]{:S(2)}, u32[]{:S(2)}) async-start(bf16[16,16,640]{2,1,0:T(8,128)(2,1)} %fusion.20), calls=%async_computation.3 | async-start | bytes 655360 | tf_op jit(solution)/shard_map/all_to_all | solution.py:113
Sparse Core Ops, SparseCore 0:
  88.9 66.6 all-gather.7
  157.5 68.1 all-gather.3
  227.5 43.1 all-gather.5
  284.5 36.2 reduce-scatter.3
where the time goes:
time: 343 us
  waiting for transfers between devices  199 us (58%)
  blocking collectives  40.7 us (12%)
  matrix products  33.2 us (10%)
  starting transfers between devices  23.6 us (7%)
  local copies, waits for them, and re-layouts  23.2 us (7%)
  between operations  13.3 us (4%)
  other arithmetic  9.27 us (3%)
    all_gather x1, waiting for transfers between devices, on_device(): portion = lax.all_gather(received, 'tensor', axis=2, tiled=True)  63.9 us
    all_gather x1, waiting for transfers between devices, side_by_side(): lax.all_gather(both, axis, axis=dim, tiled=True)  41 us
    all_to_all x1, blocking collectives, on_device(): lax.all_to_all(to_send, 'dp', split_axis=0, concat_axis=0, tiled=True)  40.7 us
    all_gather x1, waiting for transfers between devices, on_device(): lax.all_gather(shared_down, 'dp', axis=1, tiled=True)  40.7 us
    all_to_all x1, waiting for transfers between devices, copy_for_each(): return lax.all_to_all(copies, axis, split_axis=0, concat_axis=0, tiled=True)  19.5 us
    all_to_all x1, waiting for transfers between devices, sum_at_owner(): lax.all_to_all(tiles, axis, split_axis=0, concat_axis=0, tiled=True)  17.9 us
    all_to_all x1, waiting for transfers between devices, on_device(): lax.all_to_all(kept_half, 'dp', split_axis=0, concat_axis=0, tiled=True)  11.9 us
    dot_general x1, matrix products, on_device(): jnp.dot(hidden_e, expert_down, preferred_element_type=jnp.float32)  11.2 us
  transfers between devices with their start and end apart: 9, of which 8 were waited for; matrix products, arithmetic and copies ran while one was open for 14% of the time, Pallas kernels for 0%

commit v1 on v0

--- a/solution.py
+++ b/solution.py
@@ -97,7 +97,8 @@
     source_count = received.shape[0]
     slot_count = received.shape[1]
     slot_total = source_count * slot_count
-    portion = lax.all_gather(received, "tensor", axis=2, tiled=True)
+    parts = lax.all_gather(received, "tensor", axis=0, tiled=False)
+    portion = jnp.concatenate(parts, axis=2)
     flattened = portion.reshape(slot_total, portion.shape[2])
     gate_e = jnp.dot(flattened, expert_gate, preferred_element_type=jnp.float32)
     up_e = jnp.dot(flattened, expert_up, preferred_element_type=jnp.float32)

time: 343 us -> 353 us (1.029)
  local copies, waits for them, and re-layouts: 23.2 us -> 31.3 us
  waiting for transfers between devices: 199 us -> 205 us
  matrix products: 33.2 us -> 28.9 us
    all_to_all x1, waiting for transfers between devices: 17.9 us -> 29.7 us  [sum_at_owner(): lax.all_to_all(tiles, axis, split_axis=0, concat_axis=0, tiled=True)]
    all_gather x1, waiting for transfers between devices: 41 us -> 35.3 us  [side_by_side(): lax.all_gather(both, axis, axis=dim, tiled=True)]
    reshape x0 -> x1, local copies, waits for them, and re-layouts: none -> 5.51 us  [on_device(): portion = jnp.concatenate(parts, axis=2)]
    unnamed x16 -> x23, local copies, waits for them, and re-layouts: 9.48 us -> 12 us
where the time goes in v1:
time: 353 us; the launch traced here: 352 us
  waiting for transfers between devices  205 us (58%)
  blocking collectives  40.7 us (12%)
  local copies, waits for them, and re-layouts  31.3 us (9%)
  matrix products  28.9 us (8%)
  starting transfers between devices  24 us (7%)
  between operations  13.3 us (4%)
  other arithmetic  9.23 us (3%)
    all_gather x1, waiting for transfers between devices, on_device(): parts = lax.all_gather(received, 'tensor', axis=0, tiled=False)  63.9 us
    all_gather x1, waiting for transfers between devices, on_device(): lax.all_gather(shared_down, 'dp', axis=1, tiled=True)  40.7 us
    all_to_all x1, blocking collectives, on_device(): lax.all_to_all(to_send, 'dp', split_axis=0, concat_axis=0, tiled=True)  40.7 us
    all_gather x1, waiting for transfers between devices, side_by_side(): lax.all_gather(both, axis, axis=dim, tiled=True)  35.3 us
    all_to_all x1, waiting for transfers between devices, sum_at_owner(): lax.all_to_all(tiles, axis, split_axis=0, concat_axis=0, tiled=True)  29.7 us
    all_to_all x1, waiting for transfers between devices, copy_for_each(): return lax.all_to_all(copies, axis, split_axis=0, concat_axis=0, tiled=True)  19.5 us
    unnamed x23, local copies, waits for them, and re-layouts  12 us
    all_to_all x1, waiting for transfers between devices, on_device(): lax.all_to_all(kept_half, 'dp', split_axis=0, concat_axis=0, tiled=True)  11.9 us
  transfers between devices with their start and end apart: 9, of which 8 were waited for; matrix products, arithmetic and copies ran while one was open for 14% of the time, Pallas kernels for 0%

profile of v1, /device:TPU:515, one launch (start us, length us, event | category | flops | bytes accessed | tf_op | source)
XLA Modules:
  0.0 352.5 jit_solution(10060051998539844284)
XLA Ops:
  6.6 1.2 copy.14
  7.8 1.3 broadcast_in_dim.8
  9.1 7.2 %all-to-all-start = ((bf16[8,128,640]{1,2,0:T(8,128)(2,1)}), bf16[8,128,640]{1,2,0:T(8,128)(2,1)}, u32[]{:S(2)}, u32[]{:S(2)}) async-start(bf16[8,128,640]{1,2,0:T(8,128)(2,1)} %broadcast_in_dim.8), calls=%async_computation | async-start | bytes 2621440 | tf_op jit(solution)/shard_map/all_to_all | solution.py:15
  16.2 19.5 %all-to-all-done = bf16[8,128,640]{1,2,0:T(8,128)(2,1)} async-done(((bf16[8,128,640]{1,2,0:T(8,128)(2,1)}), bf16[8,128,640]{1,2,0:T(8,128)(2,1)}, u32[]{:S(2)}, u32[]{:S(2)}) %all-to-all-start) | async-done | bytes 1310752 | tf_op jit(solution)/shard_map/all_to_all | solution.py:15
  35.7 1.6 fusion.17
  37.5 8.0 %scatter_fusion = bf16[8,32,640]{2,1,0:T(8,128)(2,1)S(1)} fusion(bf16[8,32,640]{2,1,0:T(8,128)(2,1)S(1)} %broadcast_in_dim.18, s32[128]{0:T(128)S(1)} %get-tuple-element.8, bf16[128,640]{1,0:T(8,128)(2,1)S(1)} %multiply_convert_fusion), kind=kCustom, calls=%fused_computation.1 | custom fusion | bytes 492544 | tf_op jit(solution)/shard_map/scatter | solution.py:74
  45.5 40.7 %all_to_all.20 = bf16[16,16,640]{2,1,0:T(8,128)(2,1)S(1)} all-to-all(bf16[16,16,640]{2,1,0:T(8,128)(2,1)S(1)} %bitcast.66), channel_id=1, replica_groups=mesh['group'=2,'dp'=16,'tensor'=8] {'dp'}, dimensions={0} | all-to-all | bytes 655360 | tf_op jit(solution)/shard_map/all_to_all | solution.py:90
  86.2 1.6 collective-permute-done
  88.9 2.0 pad_maximum_fusion
  91.7 63.9 %all-gather.9.cloned.1.call-done = bf16[128,32,640]{2,1,0:T(8,128)(2,1)} async-done(((bf16[16,32,640]{2,1,0:T(8,128)(2,1)}), bf16[128,32,640]{2,1,0:T(8,128)(2,1)}) %all-gather.9.cloned.1.call-update) | async-done | bytes 5242896 | tf_op jit(solution)/shard_map/all_gather | solution.py:100
  155.6 5.5 %copy.15 = bf16[16,32,8,640]{3,2,1,0:T(8,128)(2,1)S(1)} copy(bf16[16,32,8,640]{3,1,0,2:T(8,128)(2,1)} %bitcast.68) | data formatting | bytes 10485760 | tf_op jit(solution)/shard_map/reshape | solution.py:101
  161.1 1.2 copy.19
  162.3 2.3 copy-done.3
  164.6 1.5 fusion.40
  166.1 11.2 %convolution_convert_fusion = bf16[512,5120]{1,0:T(8,128)(2,1)} fusion(bf16[256,5120]{1,0:T(8,128)(2,1)S(1)} %copy-done, bf16[512,5120]{1,0:T(8,128)(2,1)} %bitcast.70, bf16[5120,256]{1,0:T(8,128)(2,1)} %param.13, f32[512,256]{1,0:T(8,128)S(1)} %fusion.40), kind=kOutput, calls=%fused_computation.3 | convolution fusion | flops 2687762432 | bytes 16252928 | tf_op jit(solution)/shard_map/dot_general | solution.py:106
  177.3 3.8 %copy.20 = bf16[64,8,8,640]{3,2,1,0:T(8,128)(2,1)S(1)} copy(bf16[64,8,8,640]{3,1,2,0:T(8,128)(2,1)} %bitcast.71) | data formatting | bytes 10485760
  181.1 3.1 copy.22
  184.2 6.2 %all-to-all-start.2 = ((bf16[8,16,32,640]{3,2,1,0:T(8,128)(2,1)}), bf16[8,16,32,640]{3,2,1,0:T(8,128)(2,1)}, u32[]{:S(2)}, u32[]{:S(2)}) async-start(bf16[8,16,32,640]{3,2,1,0:T(8,128)(2,1)} %bitcast.63), calls=%async_computation.2 | async-start | bytes 10485760 | tf_op jit(solution)/shard_map/all_to_all | solution.py:38
  190.4 35.3 %all-gather.5.cloned.1.call-done = bf16[5120,1024]{1,0:T(8,128)(2,1)} async-done(((bf16[320,1024]{1,0:T(8,128)(2,1)}), bf16[5120,1024]{1,0:T(8,128)(2,1)}) %all-gather.5.cloned.1.call-update) | async-done | bytes 10485776 | tf_op jit(solution)/shard_map/all_gather | solution.py:24
  225.7 4.4 %fusion.5 = f32[128,512]{0,1:T(8,128)S(1)} fusion(bf16[128,5120]{0,1:T(8,128)(2,1)} %bitcast.1, bf16[5120,1024]{1,0:T(8,128)(2,1)} %all-gather.5.cloned.1.call-done), kind=kOutput, calls=%fused_computation.12 | convolution fusion | flops 671088640 | bytes 6815744 | tf_op jit(solution)/shard_map/dot_general | solution.py:77
  230.1 40.7 %all-gather.7.cloned.1.call-done = bf16[512,5120]{0,1:T(8,128)(2,1)} async-done(((bf16[512,320]{0,1:T(8,128)(2,1)}), bf16[512,5120]{0,1:T(8,128)(2,1)}) %all-gather.7.cloned.1.call-update) | async-done | bytes 5242896 | tf_op jit(solution)/shard_map/all_gather | solution.py:82
  270.8 10.1 %convolution_convert_fusion.1 = bf16[128,5120]{1,0:T(8,128)(2,1)S(1)} fusion(bf16[512,5120]{0,1:T(8,128)(2,1)} %all-gather.7.cloned.1.call-done, bf16[128,5120]{0,1:T(8,128)(2,1)} %bitcast.1, bf16[5120,1024]{1,0:T(8,128)(2,1)} %all-gather.5.cloned.1.call-done, f32[128,512]{0,1:T(8,128)S(1)} %fusion.5), kind=kOutput, calls=%fused_computation.4 | convolution fusion | flops 1343225856 | bytes 13369344 | tf_op jit(solution)/shard_map/dot_general | solution.py:80
  280.9 1.5 copy.17
  282.4 29.7 %all-to-all-done.2 = bf16[8,16,32,640]{3,2,1,0:T(8,128)(2,1)} async-done(((bf16[8,16,32,640]{3,2,1,0:T(8,128)(2,1)}), bf16[8,16,32,640]{3,2,1,0:T(8,128)(2,1)}, u32[]{:S(2)}, u32[]{:S(2)}) %all-to-all-start.2) | async-done | bytes 5242912 | tf_op jit(solution)/shard_map/all_to_all | solution.py:38
  312.2 3.4 convert_reduce_fusion
  316.7 2.9 collective-permute-start.1
  319.6 1.9 collective-permute-done.1
  321.4 1.9 fusion.20
  323.4 7.5 %all-to-all-start.3 = ((bf16[16,16,640]{2,1,0:T(8,128)(2,1)}), bf16[16,16,640]{2,1,0:T(8,128)(2,1)S(1)}, u32[]{:S(2)}, u32[]{:S(2)}) async-start(bf16[16,16,640]{2,1,0:T(8,128)(2,1)} %fusion.20), calls=%async_computation.3 | async-start | bytes 655360 | tf_op jit(solution)/shard_map/all_to_all | solution.py:114
  330.9 1.1 copy.18
  332.0 11.9 %all-to-all-done.3 = bf16[16,16,640]{2,1,0:T(8,128)(2,1)S(1)} async-done(((bf16[16,16,640]{2,1,0:T(8,128)(2,1)}), bf16[16,16,640]{2,1,0:T(8,128)(2,1)S(1)}, u32[]{:S(2)}, u32[]{:S(2)}) %all-to-all-start.3) | async-done | bytes 327712 | tf_op jit(solution)/shard_map/all_to_all | solution.py:114
  343.8 1.4 gather_fusion
  (35 shorter events, 4.0 us)
Async XLA Ops:
  6.5 159.6 %copy-start = (bf16[256,5120]{1,0:T(8,128)(2,1)S(1)}, bf16[256,5120]{1,0:T(8,128)(2,1)}, u32[]{:S(2)}) copy-start(bf16[256,5120]{1,0:T(8,128)(2,1)} %param.14) | copy-start | bytes 7864324
  6.6 9.7 %copy-start.6 = (s32[128]{0:T(128)S(1)}, s32[128]{0:T(128)}, u32[]{:S(2)}) copy-start(s32[128]{0:T(128)} %param.18) | copy-start | bytes 1540
  6.6 9.7 %copy-start.7 = (s32[128]{0:T(128)S(1)}, s32[128]{0:T(128)}, u32[]{:S(2)}) copy-start(s32[128]{0:T(128)} %param.19) | copy-start | bytes 1540
  6.6 29.2 %copy-start.5 = (bf16[5120,8]{0,1:T(8,128)(2,1)S(1)}, bf16[5120,8]{0,1:T(8,128)(2,1)}, u32[]{:S(2)}) copy-start(bf16[5120,8]{0,1:T(8,128)(2,1)} %param.11) | copy-start | bytes 245764
  7.8 29.5 %copy-start.4 = (bf16[128,640]{1,0:T(8,128)(2,1)S(1)}, bf16[128,640]{1,0:T(8,128)(2,1)}, u32[]{:S(2)}) copy-start(bf16[128,640]{1,0:T(8,128)(2,1)} %param.10) | copy-start | bytes 491524
  9.1 26.6 %all-to-all-start = ((bf16[8,128,640]{1,2,0:T(8,128)(2,1)}), bf16[8,128,640]{1,2,0:T(8,128)(2,1)}, u32[]{:S(2)}, u32[]{:S(2)}) async-start(bf16[8,128,640]{1,2,0:T(8,128)(2,1)} %broadcast_in_dim.8), calls=%async_computation | async-start | bytes 2621440 | tf_op jit(solution)/shard_map/all_to_all | solution.py:15
  16.2 139.4 %all-gather.9.cloned.1.call-start = ((), (), s32[]{:S(2)}) async-start(), calls=%async_computation.7 | async-start | bytes 5898240 | tf_op jit(solution)/shard_map/all_gather | solution.py:100
  86.2 1.6 collective-permute-start
  88.8 136.8 %all-gather.5.cloned.1.call-start = ((), (), s32[]{:S(2)}) async-start(), calls=%async_computation.5 | async-start | bytes 11141120 | tf_op jit(solution)/shard_map/all_gather | solution.py:24
  90.9 179.8 %all-gather.7.cloned.1.call-start = ((), (), s32[]{:S(2)}) async-start(), calls=%async_computation.6 | async-start | bytes 5570560 | tf_op jit(solution)/shard_map/all_gather | solution.py:82
  161.1 3.5 copy-start.8
  162.3 2.3 copy-start.3
  184.2 127.9 %all-to-all-start.2 = ((bf16[8,16,32,640]{3,2,1,0:T(8,128)(2,1)}), bf16[8,16,32,640]{3,2,1,0:T(8,128)(2,1)}, u32[]{:S(2)}, u32[]{:S(2)}) async-start(bf16[8,16,32,640]{3,2,1,0:T(8,128)(2,1)} %bitcast.63), calls=%async_computation.2 | async-start | bytes 10485760 | tf_op jit(solution)/shard_map/all_to_all | solution.py:38
  190.4 140.5 %reduce-scatter.4.cloned.1.call-start = ((), (), s32[]{:S(2)}) async-start(), calls=%async_computation.8 | async-start | bytes 1474560
  315.6 1.1 copy-start.2
  316.6 29.3 %copy-start.1 = (bf16[256,5120]{1,0:T(8,128)(2,1)S(1)}, bf16[256,5120]{1,0:T(8,128)(2,1)}, u32[]{:S(2)}) copy-start(bf16[256,5120]{1,0:T(8,128)(2,1)} %param.14) | copy-start | bytes 7864324
  316.7 4.7 %collective-permute-start.1 = (bf16[16,32,640]{2,1,0:T(8,128)(2,1)S(1)}, bf16[16,32,640]{2,1,0:T(8,128)(2,1)}, u32[]{:S(2)}, u32[]{:S(2)}) collective-permute-start(bf16[16,32,640]{2,1,0:T(8,128)(2,1)S(1)} %convert_element_type.53), channel_id=1, source_target_pairs={{0,8},{8,0},{16,24},{24,16},{32,40},{40,32},{48,56},{56,48},{64,72... | collective-permute-start | bytes 1966088 | tf_op jit(solution)/shard_map/ppermute | solution.py:45
  323.4 20.4 %all-to-all-start.3 = ((bf16[16,16,640]{2,1,0:T(8,128)(2,1)}), bf16[16,16,640]{2,1,0:T(8,128)(2,1)S(1)}, u32[]{:S(2)}, u32[]{:S(2)}) async-start(bf16[16,16,640]{2,1,0:T(8,128)(2,1)} %fusion.20), calls=%async_computation.3 | async-start | bytes 655360 | tf_op jit(solution)/shard_map/all_to_all | solution.py:114
Sparse Core Ops, SparseCore 0:
  89.0 66.6 all-gather.8
  157.5 68.1 all-gather.4
  227.5 43.2 all-gather.6
  282.5 41.4 reduce-scatter.3
